TPU v7x, 32 devices: a whole 2x2x4 slice. The times are simulated.
32 devices in a mesh: section: 4 (over y, x), ctx: 4 (over z), mp: 2 (over core).
Axes of the slice: x: 2, y: 2, z: 4, core: 2. Of those that a mesh axis runs over, the one named last changes fastest.
Arguments:
- head_input: bfloat16 [4, 1024, 2048], P('section', 'ctx', 'mp'), may hold values from -6 to 6
- state_proj: bfloat16 [4, 1024, 256], P('section', 'ctx'), may hold values from -6 to 6
- gate_input: bfloat16 [4, 1024, 2048], P('section', 'ctx', 'mp'), may hold values from -6 to 6
- step_raw: float32 [4, 32, 1024], P('section', 'mp', 'ctx'), may hold values from -2 to 2
- step_bias: float32 [4, 32], P('section', 'mp'), may hold values from -9.5 to -3
- decay_log: float32 [4, 32], P('section', 'mp'), may hold values from -7 to 1.5
- skip_gain: float32 [4, 32], P('section', 'mp'), may hold values from 0.5 to 1.5
- conv_head: float32 [4, 4, 2048], P('section', None, 'mp'), may hold values from -3 to 3
- conv_state: float32 [4, 4, 256], P('section'), may hold values from -3 to 3
- norm_gain: float32 [4, 2048], P('section', 'mp'), may hold values from 0.1 to 1.9
- next_weight: bfloat16 [4, 2048, 4096], P('section', 'ctx', 'mp'), may hold values from -0.125 to 0.125
Outputs:
- projected: bfloat16 [4, 1024, 4096], P('section', 'ctx', 'mp')
All inputs are finite; a program needn't handle non-finite values.
Results may differ from a plain program's by a relative error of at most 0.0087.
Values may be sent and summed in bfloat16 or wider, within the bound.
A program may use at most 64 MiB of HBM per device.

v0:
```python
import jax
import jax.numpy as jnp
from jax import lax
from jax.sharding import PartitionSpec as P

STATE = 128
BLOCK = 256
FEATURES = 2048
NORM_FLOOR = 0.25
HIGHEST = lax.Precision.HIGHEST


def from_behind(value, axis, steps):
    count = lax.axis_size(axis)
    first, last = (max(0, -steps), min(count, count - steps))
    return lax.ppermute(value, axis, [(source, source + steps) for source in range(first, last)])


def prefix(part, axis, combine, identity):
    place = lax.axis_index(axis)
    gathered = jax.tree.map(lambda a: lax.all_gather(a, axis), part)
    state = jax.tree.map(lambda a, e: jnp.zeros_like(a) + jnp.asarray(e, a.dtype), part, identity)

    def one(step, state):
        return combine(
            state, jax.tree.map(lambda a: lax.dynamic_index_in_dim(a, step, 0, False), gathered)
        )

    return lax.fori_loop(0, place, one, state)


def shifted(value, axis, steps):
    count = lax.axis_size(axis)
    pairs = [(source, (source + steps) % count) for source in range(count)]
    return lax.ppermute(value, axis, pairs)


def causal_conv(sequence, previous, weights):
    length = sequence.shape[0]
    padded = jnp.concatenate([previous, sequence], axis=0).astype(jnp.float32)
    summed = jnp.zeros(sequence.shape, jnp.float32)
    for offset in range(weights.shape[0]):
        summed = summed + weights[offset] * padded[offset : offset + length]
    return summed


def chain_step(earlier, latter):
    return (earlier[0] + latter[0], jnp.exp(latter[0])[:, None, None] * earlier[1] + latter[1])


def shards(
    head_input,
    state_proj,
    gate_input,
    step_raw,
    step_bias,
    decay_log,
    skip_gain,
    conv_head,
    conv_state,
    norm_gain,
    next_weight,
):
    tap_count = conv_head.shape[1]
    token_count = head_input.shape[1]
    local_width = head_input.shape[2]
    head_count = step_raw.shape[1]
    head_width = local_width // head_count
    block_count = token_count // BLOCK
    tails = jnp.concatenate(
        [
            head_input[0, token_count - tap_count + 1 :],
            state_proj[0, token_count - tap_count + 1 :],
        ],
        axis=1,
    )
    previous = from_behind(tails, "ctx", 1)
    conv_x = jax.nn.silu(
        causal_conv(head_input[0], previous[:, :local_width], conv_head[0])
    ).astype(jnp.bfloat16)
    conv_bc = causal_conv(state_proj[0], previous[:, local_width:], conv_state[0]).astype(
        jnp.bfloat16
    )
    blocks_x = conv_x.reshape(block_count, BLOCK, head_count, head_width)
    blocks_b = conv_bc[:, :STATE].reshape(block_count, BLOCK, STATE)
    blocks_c = conv_bc[:, STATE:].reshape(block_count, BLOCK, STATE)
    step_size = jax.nn.softplus(step_raw[0] + step_bias[0][:, None])
    log_decay = -jnp.exp(decay_log[0])[:, None] * step_size
    blocks_step = step_size.reshape(head_count, block_count, BLOCK)
    blocks_decay = log_decay.reshape(head_count, block_count, BLOCK)
    row_index = lax.broadcasted_iota(jnp.int32, (BLOCK, BLOCK), 0)
    col_index = lax.broadcasted_iota(jnp.int32, (BLOCK, BLOCK), 1)
    causal_mask = row_index >= col_index
    lower_tri = causal_mask.astype(jnp.float32)
    cumulative = jnp.einsum("hcs,ts->hct", blocks_decay, lower_tri, precision=HIGHEST)
    scores = jnp.einsum("ctn,csn->cts", blocks_c, blocks_b, preferred_element_type=jnp.float32)
    decay_diff = jnp.where(causal_mask, cumulative[..., :, None] - cumulative[..., None, :], 0.0)
    mix_weight = jnp.where(
        causal_mask, scores[None] * jnp.exp(decay_diff) * blocks_step[:, :, None, :], 0.0
    ).astype(jnp.bfloat16)
    intra_part = jnp.einsum(
        "hcts,cshp->cthp", mix_weight, blocks_x, preferred_element_type=jnp.float32
    )
    tail_weight = jnp.exp(cumulative[..., -1:] - cumulative) * blocks_step
    weighted_b = (blocks_b.astype(jnp.float32)[None] * tail_weight[..., None]).astype(jnp.bfloat16)
    updates = jnp.einsum(
        "cshp,hcsn->chpn", blocks_x, weighted_b, preferred_element_type=jnp.float32
    )
    totals = cumulative[..., -1]
    running = jnp.zeros((head_count, head_width, STATE), jnp.float32)
    before = jnp.zeros((head_count,), jnp.float32)
    entering = running
    offsets = before
    running = jnp.exp(totals[:, 0])[:, None, None] * running + updates[0]
    before = totals[:, 0]
    prior_log, prior_state = prefix(
        (before, running), "ctx", chain_step, (jnp.zeros_like(before), jnp.zeros_like(running))
    )
    full_states = jnp.stack([entering + jnp.exp(offsets)[:, None, None] * prior_state])
    inter_part = (
        jnp.einsum("ctn,chpn->cthp", blocks_c.astype(jnp.float32), full_states, precision=HIGHEST)
        * jnp.exp(cumulative).transpose(1, 2, 0)[..., None]
    )
    output = (
        intra_part + inter_part + skip_gain[0][None, None, :, None] * blocks_x.astype(jnp.float32)
    )
    gated = output.reshape(token_count, local_width) * jax.nn.silu(
        gate_input[0].astype(jnp.float32)
    )
    squares = lax.psum(jnp.sum(gated * gated, axis=1), "mp")
    mean_square = squares / FEATURES
    normed = (gated * lax.rsqrt(mean_square + NORM_FLOOR)[:, None] * norm_gain[0][None]).astype(
        jnp.bfloat16
    )
    gathered = lax.all_gather(normed, "mp", axis=1, tiled=True)
    arrived = shifted(gathered, "section", 1)
    weight_rows = next_weight[0]
    full_weight = lax.all_gather(weight_rows, "ctx", axis=0, tiled=True)
    result = jnp.dot(arrived, full_weight, preferred_element_type=jnp.float32)
    return result.astype(jnp.bfloat16)[None]


def solution(mesh):
    return jax.shard_map(
        shards,
        mesh=mesh,
        in_specs=(
            P("section", "ctx", "mp"),
            P("section", "ctx", None),
            P("section", "ctx", "mp"),
            P("section", "mp", "ctx"),
            P("section", "mp"),
            P("section", "mp"),
            P("section", "mp"),
            P("section", None, "mp"),
            P("section", None, None),
            P("section", "mp"),
            P("section", "ctx", "mp"),
        ),
        out_specs=P("section", "ctx", "mp"),
        check_vma=False,
    )
```

profile of v0, /device:TPU:0, one launch (start us, length us, event | category | flops | bytes accessed | tf_op | source)
XLA Modules:
  0.0 252.9 jit_solution(13187980075487507299)
XLA Ops:
  6.5 0.7 slice_bitcast_fusion
  7.3 0.7 slice_bitcast_fusion.1
  8.0 5.0 %collective-permute-start = (bf16[3,1280]{1,0:T(4,128)(2,1)S(1)}, bf16[3,1280]{1,0:T(4,128)(2,1)S(1)}, u32[]{:S(2)}, u32[]{:S(2)}) collective-permute-start(bf16[3,1280]{1,0:T(4,128)(2,1)S(1)} %pad_maximum_fusion), channel_id=1, source_target_pairs={{0,2},{2,4},{4,6},{1,3},{3,5},{5,7},{8,10},{10,12},{12,14},{9,11},... | collective-permute-start | bytes 23048 | tf_op jit(solution)/shard_map/ppermute | solution.py:16
  12.9 0.9 fusion.44
  13.8 0.7 negate_bitcast_fusion
  14.5 0.8 compare_select_fusion
  15.7 0.8 exponential_bitcast_fusion.1
  16.6 0.8 fusion.45
  17.4 1.2 copy.20
  18.9 0.9 maximum_convert_fusion.1
  20.4 1.6 multiply_convert_fusion.2
  22.0 1.6 convolution_add_fusion
  23.7 0.7 dynamic-slice
  25.3 10.0 %all-reduce = f32[64]{0:T(128)S(1)} all-reduce(f32[64]{0:T(128)S(1)} %dynamic-update-slice), channel_id=2, replica_groups=mesh['section'=4,'ctx'=4,'mp'=2] {'ctx'}, use_global_device_ids=true, to_apply=%add | all-reduce | flops 64 | bytes 512
  35.8 33.8 %all-gather.9.cloned.1.call-done = f32[64,64,128]{2,1,0:T(8,128)} async-done(((f32[16,64,128]{2,1,0:T(8,128)}), f32[64,64,128]{2,1,0:T(8,128)}) %all-gather.9.cloned.1.call-update) | async-done | bytes 2097168 | tf_op jit(solution)/shard_map/all_gather | solution.py:21
  70.4 1.6 multiply_reduce_fusion
  72.0 2.5 psum.7
  74.5 1.2 fusion.30
  75.7 0.7 all-gather.11.cloned.1.call-update
  76.4 10.9 %all-gather.7.cloned.1.call-done = bf16[256,2048]{0,1:T(8,128)(2,1)} async-done(((bf16[256,1024]{0,1:T(8,128)(2,1)}), bf16[256,2048]{0,1:T(8,128)(2,1)}) %all-gather.7.cloned.1.call-update) | async-done | bytes 1048592 | tf_op jit(solution)/shard_map/all_gather | solution.py:135
  87.3 1.7 collective-permute-start.1
  89.0 24.7 %collective-permute-done.1 = bf16[256,2048]{0,1:T(8,128)(2,1)S(1)} collective-permute-done((bf16[256,2048]{0,1:T(8,128)(2,1)}, bf16[256,2048]{0,1:T(8,128)(2,1)S(1)}, u32[]{:S(2)}, u32[]{:S(2)}) %collective-permute-start.1) | collective-permute-done | bytes 1048608 | tf_op jit(solution)/shard_map/ppermute | solution.py:35
  113.8 125.9 %all-gather.11.cloned.1.call-done = bf16[1,2048,2048]{2,1,0:T(8,128)(2,1)} async-done(((bf16[1,512,2048]{2,1,0:T(8,128)(2,1)}), bf16[1,2048,2048]{2,1,0:T(8,128)(2,1)}) %all-gather.11.cloned.1.call-update) | async-done | bytes 8388624 | tf_op jit(solution)/shard_map/all_gather | solution.py:138
  239.7 6.7 %fusion.5 = bf16[1,256,2048]{2,1,0:T(8,128)(2,1)} fusion(bf16[256,2048]{0,1:T(8,128)(2,1)S(1)} %collective-permute-done.1, bf16[1,2048,2048]{2,1,0:T(8,128)(2,1)} %all-gather.11.cloned.1.call-done), kind=kOutput, calls=%fused_computation.6 | convolution fusion | flops 2148007936 | bytes 10485760 | tf_op jit(solution)/shard_map/dot_general | solution.py:139
  (33 shorter events, 2.7 us)
Async XLA Ops:
  6.5 63.1 %all-gather.9.cloned.1.call-start = ((), (), s32[]{:S(2)}) async-start(), calls=%async_computation.1 | async-start | bytes 2621440 | tf_op jit(solution)/shard_map/all_gather | solution.py:21
  8.0 10.7 %collective-permute-start = (bf16[3,1280]{1,0:T(4,128)(2,1)S(1)}, bf16[3,1280]{1,0:T(4,128)(2,1)S(1)}, u32[]{:S(2)}, u32[]{:S(2)}) collective-permute-start(bf16[3,1280]{1,0:T(4,128)(2,1)S(1)} %pad_maximum_fusion), channel_id=1, source_target_pairs={{0,2},{2,4},{4,6},{1,3},{3,5},{5,7},{8,10},{10,12},{12,14},{9,11},... | collective-permute-start | bytes 23048 | tf_op jit(solution)/shard_map/ppermute | solution.py:16
  20.0 3.7 %copy-start.3 = (u32[32]{0:T(128)S(1)}, u32[32]{0:T(128)}, u32[]{:S(2)}) copy-start(u32[32]{0:T(128)} %constant.51) | copy-start | bytes 388
  20.0 15.4 %copy-start = (bf16[1,256,1024]{2,1,0:T(8,128)(2,1)S(1)}, bf16[1,256,1024]{2,1,0:T(8,128)(2,1)}, u32[]{:S(2)}) copy-start(bf16[1,256,1024]{2,1,0:T(8,128)(2,1)} %param.15) | copy-start | bytes 1572868
  23.6 63.7 %all-gather.7.cloned.1.call-start = ((), (), s32[]{:S(2)}) async-start(), calls=%async_computation | async-start | bytes 1572864 | tf_op jit(solution)/shard_map/all_gather | solution.py:135
  69.7 0.7 copy-start.2
  70.4 4.1 %copy-start.1 = (f32[1,1024]{1,0:T(1,128)S(1)}, f32[1,1024]{1,0:T(1,128)}, u32[]{:S(2)}) copy-start(f32[1,1024]{1,0:T(1,128)} %param.22) | copy-start | bytes 12292
  75.7 164.0 %all-gather.11.cloned.1.call-start = ((), (), s32[]{:S(2)}) async-start(), calls=%async_computation.2 | async-start | bytes 10485760 | tf_op jit(solution)/shard_map/all_gather | solution.py:138
  87.3 26.5 %collective-permute-start.1 = (bf16[256,2048]{0,1:T(8,128)(2,1)}, bf16[256,2048]{0,1:T(8,128)(2,1)S(1)}, u32[]{:S(2)}, u32[]{:S(2)}) collective-permute-start(bf16[256,2048]{0,1:T(8,128)(2,1)} %all-gather.7.cloned.1.call-done), channel_id=1, source_target_pairs={{0,8},{8,16},{16,24},{24,0},{1,9},{9,17},{17,25},{25,1},{2,10},{10... | collective-permute-start | bytes 3145736 | tf_op jit(solution)/shard_map/ppermute | solution.py:35
Sparse Core Ops, SparseCore 0:
  23.7 45.8 all-gather.8
  75.8 11.4 all-gather.6
  88.9 150.7 all-gather.10
where the time goes:
time: 254 us; the launch traced here: 253 us
  waiting for transfers between devices  196 us (77%)
  between operations  14 us (6%)
  blocking collectives  12.5 us (5%)
  matrix products  10.9 us (4%)
  other arithmetic  6.79 us (3%)
  starting transfers between devices  6.78 us (3%)
  local copies, waits for them, and re-layouts  5.88 us (2%)
    all_gather x1, waiting for transfers between devices, shards(): full_weight = lax.all_gather(weight_rows, 'ctx', axis=0, tiled=True)  126 us
    all_gather x1, waiting for transfers between devices, prefix(): gathered = jax.tree.map(lambda a: lax.all_gather(a, axis), part)  33.8 us
    ppermute x1, waiting for transfers between devices, shifted(): return lax.ppermute(value, axis, pairs)  24.7 us
    all_gather x1, waiting for transfers between devices, shards(): gathered = lax.all_gather(normed, 'mp', axis=1, tiled=True)  10.9 us
    unnamed x1, blocking collectives  10 us
    dot_general x1, matrix products, shards(): result = jnp.dot(arrived, full_weight, preferred_element_type=jnp.float32)  6.7 us
  transfers between devices with their start and end apart: 5, of which 4 were waited for; matrix products, arithmetic and copies ran while one was open for 3% of the time, Pallas kernels for 0%

commit v1 on v0

--- a/solution.py
+++ b/solution.py
@@ -61,6 +61,20 @@
     norm_gain,
     next_weight,
 ):
+
+    def get_the_types(row_data):
+        ndev = lax.axis_size("ctx")
+        made = [row_data]
+        for k in range(ndev - 1):
+            made.append(
+                lax.ppermute(made[-1], "ctx", [(k0, (k0 + 1) % ndev) for k0 in range(ndev)])
+            )
+        return jnp.roll(
+            jnp.concatenate(made[::-1], axis=0),
+            (lax.axis_index("ctx") + 1) * row_data.shape[0],
+            axis=0,
+        )
+
     tap_count = conv_head.shape[1]
     token_count = head_input.shape[1]
     local_width = head_input.shape[2]
@@ -135,7 +149,7 @@
     gathered = lax.all_gather(normed, "mp", axis=1, tiled=True)
     arrived = shifted(gathered, "section", 1)
     weight_rows = next_weight[0]
-    full_weight = lax.all_gather(weight_rows, "ctx", axis=0, tiled=True)
+    full_weight = get_the_types(weight_rows)
     result = jnp.dot(arrived, full_weight, preferred_element_type=jnp.float32)
     return result.astype(jnp.bfloat16)[None]
 

time: 254 us -> 236 us (0.929)
  waiting for transfers between devices: 196 us -> 118 us
  blocking collectives: 12.5 us -> 51.1 us
  local copies, waits for them, and re-layouts: 5.88 us -> 19.1 us
  starting transfers between devices: 6.78 us -> 12.2 us
  other arithmetic: 6.79 us -> 10.7 us
    all_gather x1 -> x0, waiting for transfers between devices: 126 us -> none  [shards(): full_weight = lax.all_gather(weight_rows, 'ctx', axis=0, tiled=True)]
    ppermute x0 -> x3, waiting for transfers between devices: none -> 107 us  [get_the_types(): lax.ppermute(made[-1], 'ctx', [(k0, (k0 + 1) % ndev) for k0 in range(ndev)])]
    unnamed x1, blocking collectives: 10 us -> 48.7 us
    all_gather x1, waiting for transfers between devices: 33.8 us -> 0.02 us  [prefix(): gathered = jax.tree.map(lambda a: lax.all_gather(a, axis), part)]
    ppermute x1, waiting for transfers between devices: 24.7 us -> 0.01 us  [shifted(): return lax.ppermute(value, axis, pairs)]
    unnamed x13 -> x34, local copies, waits for them, and re-layouts: 2.39 us -> 14.3 us
    ppermute x0 -> x3, starting transfers between devices: none -> 5.44 us  [get_the_types(): lax.ppermute(made[-1], 'ctx', [(k0, (k0 + 1) % ndev) for k0 in range(ndev)])]
    dot_general x1, matrix products: 6.7 us -> 3.32 us  [shards(): result = jnp.dot(arrived, full_weight, preferred_element_type=jnp.float32)]
  transfers between devices with their start and end apart: 5 -> 7, of which waited for: 4 -> 3; matrix products, arithmetic and copies ran while one was open for 3% -> 12% of each run, Pallas kernels for 0% -> 0%
where the time goes in v1:
time: 236 us; the launch traced here: 235 us
  waiting for transfers between devices  118 us (50%)
  blocking collectives  51.1 us (22%)
  local copies, waits for them, and re-layouts  19.1 us (8%)
  between operations  14.4 us (6%)
  starting transfers between devices  12.2 us (5%)
  other arithmetic  10.7 us (5%)
  matrix products  9.68 us (4%)
    ppermute x3, waiting for transfers between devices, get_the_types(): lax.ppermute(made[-1], 'ctx', [(k0, (k0 + 1) % ndev) for k0 in range(ndev)])  107 us
    unnamed x1, blocking collectives  48.7 us
    unnamed x34, local copies, waits for them, and re-layouts  14.3 us
    all_gather x1, waiting for transfers between devices, shards(): gathered = lax.all_gather(normed, 'mp', axis=1, tiled=True)  11.2 us
    ppermute x3, starting transfers between devices, get_the_types(): lax.ppermute(made[-1], 'ctx', [(k0, (k0 + 1) % ndev) for k0 in range(ndev)])  5.44 us
    ppermute x1, starting transfers between devices, from_behind(): lax.ppermute(value, axis, [(source, source + steps) for source in range(f...  4.96 us
  transfers between devices with their start and end apart: 7, of which 3 were waited for; matrix products, arithmetic and copies ran while one was open for 12% of the time, Pallas kernels for 0%

profile of v1, /device:TPU:0, one launch (start us, length us, event | category | flops | bytes accessed | tf_op | source)
XLA Modules:
  0.0 235.1 jit_solution(10748900070266905472)
XLA Ops:
  8.0 5.0 %collective-permute-start = (bf16[3,1280]{1,0:T(4,128)(2,1)S(1)}, bf16[3,1280]{1,0:T(4,128)(2,1)S(1)}, u32[]{:S(2)}, u32[]{:S(2)}) collective-permute-start(bf16[3,1280]{1,0:T(4,128)(2,1)S(1)} %pad_maximum_fusion), channel_id=1, source_target_pairs={{0,2},{2,4},{4,6},{1,3},{3,5},{5,7},{8,10},{10,12},{12,14},{9,11},... | collective-permute-start | bytes 23048 | tf_op jit(solution)/shard_map/ppermute | solution.py:16
  15.5 1.5 fusion.45
  16.9 1.4 exponential_bitcast_fusion.1
  19.2 1.2 copy.20
  20.7 0.9 maximum_convert_fusion.1
  22.2 2.5 %multiply_convert_fusion.2 = bf16[256,1024]{0,1:T(8,128)(2,1)S(1)} fusion(f32[259,1024]{0,1:T(8,128)S(1)} %maximum_convert_fusion, f32[1024]{0:T(1024)} %bitcast.103, f32[1024]{0:T(1024)} %bitcast.104, f32[1024]{0:T(1024)} %bitcast.102, f32[1024]{0:T(1024)} %bitcast.101), kind=kLoop, calls=%fused_computation.40 | loop fusion | flops 3145728 | bytes 4734976 | tf_op jit(solution)/shard_map/convert_element_type | solution.py:94
  25.6 1.6 convolution_add_fusion
  27.3 1.6 collective-permute-start.2
  28.9 81.2 %collective-permute-done.2 = bf16[512,2048]{1,0:T(8,128)(2,1)} collective-permute-done((bf16[512,2048]{1,0:T(8,128)(2,1)S(1)}, bf16[512,2048]{1,0:T(8,128)(2,1)}, u32[]{:S(2)}, u32[]{:S(2)}) %collective-permute-start.2) | collective-permute-done | bytes 2097184 | tf_op jit(solution)/shard_map/ppermute | solution.py:70
  111.7 48.7 %all-reduce = f32[64]{0:T(128)S(1)} all-reduce(f32[64]{0:T(128)S(1)} %dynamic-update-slice), channel_id=2, replica_groups=mesh['section'=4,'ctx'=4,'mp'=2] {'ctx'}, use_global_device_ids=true, to_apply=%add | all-reduce | flops 64 | bytes 512
  162.8 3.8 %collective-permute-start.4 = (bf16[512,2048]{1,0:T(8,128)(2,1)}, bf16[512,2048]{1,0:T(8,128)(2,1)}, u32[]{:S(2)}, u32[]{:S(2)}) collective-permute-start(bf16[512,2048]{1,0:T(8,128)(2,1)} %collective-permute-done.3), channel_id=1, source_target_pairs={{0,2},{2,4},{4,6},{6,0},{1,3},{3,5},{5,7},{7,1},{8,10},{10,12},{12... | collective-permute-start | bytes 6291464 | tf_op jit(solution)/shard_map/ppermute | solution.py:70
  166.7 3.8 %multiply_reduce_fusion = (f32[256]{0:T(256)S(1)}, f32[1,256,16,64]{1,3,2,0:T(8,128)}) fusion(bf16[1,256,16,64]{1,3,2,0:T(8,128)(2,1)} %bitcast.98, f32[16]{0:T(128)} %bitcast.112, f32[1,256,16,64]{1,3,2,0:T(8,128)S(1)} %fusion.16, bf16[256,16,64]{0,2,1:T(8,128)(2,1)} %bitcast.97, f32[16,256]{1,0:T(8,128)} %copy-done.4, f32[16,256]{1,0:T(8,128)} %copy-done.3, ...), kind=kOutput, calls=%fused_computation.37 | convolution fusion | flops 143654656 | bytes 4031552 | tf_op jit(solution)/shard_map/hcts,cshp->cthp/dot_general | solution.py:115
  170.4 2.4 %psum.7 = f32[256]{0:T(256)S(1)} all-reduce(f32[256]{0:T(256)S(1)} %get-tuple-element.72), channel_id=1, replica_groups=mesh['section'=4,'ctx'=4,'mp'=2] {'mp'}, use_global_device_ids=true, to_apply=%region_3.4 | all-reduce | flops 256 | bytes 2048 | tf_op jit(solution)/shard_map/psum | solution.py:144
  172.9 2.4 %fusion.30 = bf16[256,1024]{0,1:T(8,128)(2,1)} fusion(f32[1,256,16,64]{1,3,2,0:T(8,128)} %get-tuple-element.73, f32[1024]{0:T(1024)S(1)} %bitcast.105, f32[256]{0:T(256)S(1)} %add_rsqrt_fusion, bf16[1,256,1024]{1,2,0:T(8,128)(2,1)S(1)} %copy.22), kind=kLoop, calls=%fused_computation.41 | loop fusion | flops 2359296 | bytes 2102272 | tf_op jit(solution)/shard_map/convert_element_type | solution.py:146
  175.3 11.2 %all-gather.5.cloned.1.call-done = bf16[256,2048]{0,1:T(8,128)(2,1)} async-done(((bf16[256,1024]{0,1:T(8,128)(2,1)}), bf16[256,2048]{0,1:T(8,128)(2,1)}) %all-gather.5.cloned.1.call-update) | async-done | bytes 1048592 | tf_op jit(solution)/shard_map/all_gather | solution.py:149
  186.5 1.7 collective-permute-start.1
  188.2 25.4 %collective-permute-done.4 = bf16[512,2048]{1,0:T(8,128)(2,1)} collective-permute-done((bf16[512,2048]{1,0:T(8,128)(2,1)}, bf16[512,2048]{1,0:T(8,128)(2,1)}, u32[]{:S(2)}, u32[]{:S(2)}) %collective-permute-start.4) | collective-permute-done | bytes 2097184 | tf_op jit(solution)/shard_map/ppermute | solution.py:70
  213.6 1.8 constant_dynamic-update-slice_fusion.7
  215.4 1.8 constant_dynamic-update-slice_fusion.6
  217.3 1.8 constant_dynamic-update-slice_fusion.5
  219.3 1.8 constant_dynamic-update-slice_fusion.3
  221.1 1.8 constant_dynamic-update-slice_fusion.2
  222.9 1.8 constant_dynamic-update-slice_fusion.1
  224.9 3.3 %fusion.5 = bf16[1,256,2048]{2,1,0:T(8,128)(2,1)} fusion(bf16[256,2048]{0,1:T(8,128)(2,1)S(1)} %collective-permute-done.1, bf16[4096,2048]{1,0:T(8,128)(2,1)S(1)} %constant_dynamic-update-slice_fusion, s32[]{:T(128)S(6)} %select_n.46), kind=kOutput, calls=%fused_computation.6 | convolution fusion | flops 2148007936 | bytes 10485764 | tf_op jit(solution)/shard_map/dot_general | solution.py:153
  (58 shorter events, 10.0 us)
Async XLA Ops:
  6.5 155.6 %all-gather.7.cloned.1.call-start = ((), (), s32[]{:S(2)}) async-start(), calls=%async_computation.1 | async-start | bytes 2621440 | tf_op jit(solution)/shard_map/all_gather | solution.py:21
  8.0 12.5 %collective-permute-start = (bf16[3,1280]{1,0:T(4,128)(2,1)S(1)}, bf16[3,1280]{1,0:T(4,128)(2,1)S(1)}, u32[]{:S(2)}, u32[]{:S(2)}) collective-permute-start(bf16[3,1280]{1,0:T(4,128)(2,1)S(1)} %pad_maximum_fusion), channel_id=1, source_target_pairs={{0,2},{2,4},{4,6},{1,3},{3,5},{5,7},{8,10},{10,12},{12,14},{9,11},... | collective-permute-start | bytes 23048 | tf_op jit(solution)/shard_map/ppermute | solution.py:16
  14.4 7.4 %copy-start.4 = (f32[16,256]{1,0:T(8,128)}, f32[16,256]{1,0:T(8,128)S(1)}, u32[]{:S(2)}) copy-start(f32[16,256]{1,0:T(8,128)S(1)} %compare_select_fusion) | copy-start | bytes 49156
  14.6 7.2 %copy-start.3 = (f32[16,256]{1,0:T(8,128)}, f32[16,256]{1,0:T(8,128)S(1)}, u32[]{:S(2)}) copy-start(f32[16,256]{1,0:T(8,128)S(1)} %fusion.35) | copy-start | bytes 49156
  15.5 6.4 %copy-start.7 = (f32[16]{0:T(128)}, f32[16]{0:T(128)S(1)}, u32[]{:S(2)}) copy-start(f32[16]{0:T(128)S(1)} %get-tuple-element.51) | copy-start | bytes 196
  21.6 3.9 %copy-start.5 = (f32[16,256]{1,0:T(8,128)S(1)}, f32[16,256]{1,0:T(8,128)}, u32[]{:S(2)}) copy-start(f32[16,256]{1,0:T(8,128)} %get-tuple-element.63) | copy-start | bytes 49156
  21.7 3.9 %copy-start.9 = (f32[16]{0:T(128)S(1)}, f32[16]{0:T(128)}, u32[]{:S(2)}) copy-start(f32[16]{0:T(128)} %get-tuple-element.50) | copy-start | bytes 196
  21.8 5.4 %copy-start = (bf16[1,512,2048]{2,1,0:T(8,128)(2,1)S(1)}, bf16[1,512,2048]{2,1,0:T(8,128)(2,1)}, u32[]{:S(2)}) copy-start(bf16[1,512,2048]{2,1,0:T(8,128)(2,1)} %param.23) | copy-start | bytes 6291460
  21.9 139.2 %copy-start.2 = (bf16[1,256,1024]{2,1,0:T(8,128)(2,1)S(1)}, bf16[1,256,1024]{2,1,0:T(8,128)(2,1)}, u32[]{:S(2)}) copy-start(bf16[1,256,1024]{2,1,0:T(8,128)(2,1)} %param.15) | copy-start | bytes 1572868
  22.2 87.9 %copy-start.10 = (u32[32]{0:T(128)S(1)}, u32[32]{0:T(128)}, u32[]{:S(2)}) copy-start(u32[32]{0:T(128)} %constant.76) | copy-start | bytes 388
  22.2 89.3 %copy-start.8 = (f32[16]{0:T(128)S(1)}, f32[16]{0:T(128)}, u32[]{:S(2)}) copy-start(f32[16]{0:T(128)} %copy-done.7) | copy-start | bytes 196
  24.8 0.8 copy-start.1
  27.2 159.3 %all-gather.5.cloned.1.call-start = ((), (), s32[]{:S(2)}) async-start(), calls=%async_computation | async-start | bytes 1572864 | tf_op jit(solution)/shard_map/all_gather | solution.py:149
  27.3 82.8 %collective-permute-start.2 = (bf16[512,2048]{1,0:T(8,128)(2,1)S(1)}, bf16[512,2048]{1,0:T(8,128)(2,1)}, u32[]{:S(2)}, u32[]{:S(2)}) collective-permute-start(bf16[512,2048]{1,0:T(8,128)(2,1)S(1)} %bitcast.92), channel_id=1, source_target_pairs={{0,2},{2,4},{4,6},{6,0},{1,3},{3,5},{5,7},{7,1},{8,10},{10,12},{12... | collective-permute-start | bytes 6291464 | tf_op jit(solution)/shard_map/ppermute | solution.py:70
  110.1 52.7 %collective-permute-start.3 = (bf16[512,2048]{1,0:T(8,128)(2,1)}, bf16[512,2048]{1,0:T(8,128)(2,1)}, u32[]{:S(2)}, u32[]{:S(2)}) collective-permute-start(bf16[512,2048]{1,0:T(8,128)(2,1)} %collective-permute-done.2), channel_id=1, source_target_pairs={{0,2},{2,4},{4,6},{6,0},{1,3},{3,5},{5,7},{7,1},{8,10},{10,12},{12... | collective-permute-start | bytes 6291464 | tf_op jit(solution)/shard_map/ppermute | solution.py:70
  162.8 50.7 %collective-permute-start.4 = (bf16[512,2048]{1,0:T(8,128)(2,1)}, bf16[512,2048]{1,0:T(8,128)(2,1)}, u32[]{:S(2)}, u32[]{:S(2)}) collective-permute-start(bf16[512,2048]{1,0:T(8,128)(2,1)} %collective-permute-done.3), channel_id=1, source_target_pairs={{0,2},{2,4},{4,6},{6,0},{1,3},{3,5},{5,7},{7,1},{8,10},{10,12},{12... | collective-permute-start | bytes 6291464 | tf_op jit(solution)/shard_map/ppermute | solution.py:70
  166.6 6.3 %copy-start.6 = (f32[1,1024]{1,0:T(1,128)S(1)}, f32[1,1024]{1,0:T(1,128)}, u32[]{:S(2)}) copy-start(f32[1,1024]{1,0:T(1,128)} %param.22) | copy-start | bytes 12292
  186.5 38.4 %collective-permute-start.1 = (bf16[256,2048]{0,1:T(8,128)(2,1)}, bf16[256,2048]{0,1:T(8,128)(2,1)S(1)}, u32[]{:S(2)}, u32[]{:S(2)}) collective-permute-start(bf16[256,2048]{0,1:T(8,128)(2,1)} %all-gather.5.cloned.1.call-done), channel_id=1, source_target_pairs={{0,8},{8,16},{16,24},{24,0},{1,9},{9,17},{17,25},{25,1},{2,10},{10... | collective-permute-start | bytes 3145736 | tf_op jit(solution)/shard_map/ppermute | solution.py:35
Sparse Core Ops, SparseCore 0:
  27.3 80.2 all-gather.6
  175.4 11.0 all-gather.4
